TPU v7x, 32 devices: a whole 2x2x4 slice. The times are simulated.
32 devices in a mesh: groups: 2 (over x), lon: 8 (over z, y), lat: 2 (over core).
Axes of the slice: x: 2, y: 2, z: 4, core: 2. Of those that a mesh axis runs over, the one named last changes fastest.
Arguments:
- fields: bfloat16 [24, 1024, 128], P(('groups', 'lat'), 'lon'), parts along dimension 0, may hold values from -6 to 6
- norm_gain: float32 [128], replicated, may hold values from 0.5 to 1.5
- w_qkv: bfloat16 [128, 384], replicated, may hold values from -5.303301 to 5.303301
- w_out: bfloat16 [128, 128], replicated, may hold values from -0.5 to 0.5
Outputs:
- updated: bfloat16 [24, 1024, 128], P(('groups', 'lat'), 'lon'), parts along dimension 0
There are 2 independent parts, one for each index of `groups`. A program takes and returns all parts, laid end to end along the dimension named above; an argument that names none is the same for every part. Nothing has to cross between parts.
All inputs are finite; a program needn't handle non-finite values.
Results may differ from a plain program's by a relative error of at most 0.005.
The roundings to bfloat16 on the way count: a program that leaves them out, or rounds other values in their place, can miss the bound.
Values may be sent and summed in bfloat16 or wider, within the bound.
A program may use at most 128 MiB of HBM per device.

v0:
```python
import math

import jax
import jax.numpy as jnp
from jax import lax
from jax.sharding import PartitionSpec as P

HEADS = 8


def attend_items(local):
    total_cells = local.shape[2]
    head_width = local.shape[3] // 3
    block = math.gcd(total_cells, 512)

    def one_item(item):
        item_keys = item[:, head_width : 2 * head_width]
        item_values = item[:, 2 * head_width :]
        query_blocks = item[:, :head_width].reshape(total_cells // block, block, head_width)

        def one_block(query_block):
            scores = jnp.dot(query_block, item_keys.T, preferred_element_type=jnp.float32)
            highest = jnp.max(scores, axis=-1, keepdims=True)
            expd = jnp.exp(scores - highest)
            totals = jnp.sum(expd, axis=-1, keepdims=True)
            mixed = jnp.dot(
                expd.astype(jnp.bfloat16), item_values, preferred_element_type=jnp.float32
            )
            return (mixed / totals).astype(jnp.bfloat16)

        return lax.map(one_block, query_blocks).reshape(total_cells, head_width)

    flat = local.reshape(local.shape[0] * local.shape[1], total_cells, 3 * head_width)
    results = lax.map(one_item, flat)
    return results.reshape(local.shape[0], local.shape[1], total_cells, head_width)


def body(fields, norm_gain, w_qkv, w_out):
    lat_rows, lon_cells, width = fields.shape
    head_count = HEADS
    head_width = width // head_count
    inputs = fields.astype(jnp.float32)
    center = jnp.mean(inputs, axis=-1, keepdims=True)
    spread = jnp.mean((inputs - center) ** 2, axis=-1, keepdims=True)
    normed = ((inputs - center) * lax.rsqrt(spread + 1e-05) * norm_gain).astype(jnp.bfloat16)
    projected = jnp.dot(normed.reshape(-1, width), w_qkv, preferred_element_type=jnp.float32)
    projected = projected.reshape(lat_rows, lon_cells, 3 * width)
    queries = (projected[..., :width] * (1.0 / math.sqrt(head_width))).astype(jnp.bfloat16)
    queries = queries.reshape(lat_rows, lon_cells, head_count, head_width)
    cycle_size = lax.axis_size("lon")
    key_part = (
        projected[..., width : 2 * width]
        .astype(jnp.bfloat16)
        .reshape(lat_rows, lon_cells, head_count, head_width)
    )
    value_part = (
        projected[..., 2 * width :]
        .astype(jnp.bfloat16)
        .reshape(lat_rows, lon_cells, head_count, head_width)
    )
    stacked = jnp.concatenate([queries, key_part, value_part], axis=-1)
    per_device = lat_rows * head_count // cycle_size
    stacked = jnp.transpose(stacked, (0, 2, 1, 3)).reshape(
        cycle_size, per_device, lon_cells, 3 * head_width
    )
    results = attend_items(lax.all_to_all(stacked, "lon", split_axis=0, concat_axis=2, tiled=True))
    returned = lax.all_to_all(results, "lon", split_axis=2, concat_axis=0, tiled=True)
    returned = returned.reshape(lat_rows, head_count, lon_cells, head_width)
    attended = jnp.transpose(returned, (0, 2, 1, 3)).reshape(lat_rows * lon_cells, width)
    output = jnp.dot(attended, w_out, preferred_element_type=jnp.float32)
    return (inputs + output.reshape(lat_rows, lon_cells, width)).astype(jnp.bfloat16)


def solution(mesh):
    return jax.shard_map(
        body,
        mesh=mesh,
        in_specs=(P(("groups", "lat"), "lon", None), P(), P(), P()),
        out_specs=P(("groups", "lat"), "lon", None),
        check_vma=False,
    )
```

profile of v0, /device:TPU:0, one launch (start us, length us, event | category | flops | bytes accessed | tf_op | source)
XLA Modules:
  0.0 70.3 jit_solution(3811145601914124028)
XLA Ops:
  0.0 1.1 %convert_reduce_fusion = f32[6,128]{1,0:T(8,128)S(1)} fusion(bf16[6,128,128]{2,1,0:T(8,128)(2,1)} %param.8), kind=kLoop, calls=%fused_computation.18 | loop fusion | flops 195840 | bytes 199680 | tf_op jit(solution)/shard_map/reduce_sum | solution.py:43
  1.1 1.2 %fusion.14 = f32[6,128]{1,0:T(8,128)S(1)} fusion(bf16[6,128,128]{2,1,0:T(8,128)(2,1)} %param.8, f32[6,128]{1,0:T(8,128)S(1)} %broadcast_multiply_fusion), kind=kLoop, calls=%fused_computation.22 | loop fusion | flops 392448 | bytes 202752 | tf_op jit(solution)/shard_map/reduce_sum | solution.py:44
  2.4 1.4 %fusion.28 = (bf16[6,128,384]{2,1,0:T(8,128)(2,1)S(1)}, f32[6,128,384]{2,1,0:T(8,128)S(1)}) fusion(bf16[128,384]{1,0:T(8,128)(2,1)S(1)} %copy-done, bf16[6,128,128]{2,1,0:T(8,128)(2,1)} %param.8, f32[128]{0:T(128)} %param.9, f32[6,128]{1,0:T(8,128)S(1)} %add_rsqrt_fusion, f32[6,128]{1,0:T(8,128)S(1)} %broadcast_multiply_fusion), kind=kOutput, calls=%fused_computation.38 | convolution fusion | flops 76283904 | bytes 2071040 | tf_op jit(solution)/shard_map/dot_general | solution.py:46
  3.7 0.1 fusion.27
  3.8 0.2 copy.23
  4.0 0.2 copy.24
  4.2 0.2 copy.22
  4.4 0.9 %pad_maximum_fusion = bf16[6,128,8,48]{1,3,2,0:T(8,128)(2,1)} fusion(bf16[6,128,8,16]{1,3,2,0:T(8,128)(2,1)S(1)} %bitcast.72, bf16[6,128,8,16]{1,3,2,0:T(8,128)(2,1)S(1)} %bitcast.71, bf16[6,128,8,16]{1,3,2,0:T(8,128)(2,1)S(1)} %bitcast.73), kind=kLoop, calls=%fused_computation.19 | loop fusion | flops 1769472 | bytes 1179648 | tf_op jit(solution)/shard_map/concatenate | solution.py:61
  5.3 7.3 %all-to-all-start = ((bf16[8,6,128,48]{2,3,1,0:T(8,128)(2,1)}), bf16[8,6,128,48]{2,3,1,0:T(8,128)(2,1)S(1)}, u32[]{:S(2)}, u32[]{:S(2)}) async-start(bf16[8,6,128,48]{2,3,1,0:T(8,128)(2,1)} %bitcast.8), calls=%async_computation | async-start | bytes 1179648 | tf_op jit(solution)/shard_map/all_to_all | solution.py:66
  12.6 15.9 %all-to-all-done = bf16[8,6,128,48]{2,3,1,0:T(8,128)(2,1)S(1)} async-done(((bf16[8,6,128,48]{2,3,1,0:T(8,128)(2,1)}), bf16[8,6,128,48]{2,3,1,0:T(8,128)(2,1)S(1)}, u32[]{:S(2)}, u32[]{:S(2)}) %all-to-all-start) | async-done | bytes 589856 | tf_op jit(solution)/shard_map/all_to_all | solution.py:66
  28.5 0.2 copy.25
  28.7 0.3 reshape.55
  29.0 19.6 %while.21 = (s32[]{:T(128)}, bf16[6,1024,16]{1,2,0:T(8,128)(2,1)S(1)}, bf16[6,1024,48]{1,2,0:T(8,128)(2,1)S(1)}, s32[]{:T(128)}, s32[]{:T(128)}, /*index=5*/s32[]{:T(128)}) while((s32[]{:T(128)}, bf16[6,1024,16]{1,2,0:T(8,128)(2,1)S(1)}, bf16[6,1024,48]{1,2,0:T(8,128)(2,1)S(1)}, s32[]{:T(128)}, s32[]{:T(128)}, /*index=5*/s32[]{:T(128)}) %tuple.49), condition=%wide.region_7.8_spmd, body=%wide.region_2.7_spmd.sunk | while | flops 36191232 | bytes 7055570 | solution.py:34
  29.0 3.1 %while.22 = (s32[]{:T(128)}, bf16[2,512,16]{1,2,0:T(8,128)(2,1)S(1)}, bf16[2,512,16]{1,2,0:T(8,128)(2,1)S(1)}, bf16[1024,16]{0,1:T(8,128)(2,1)S(1)}, bf16[1024,16]{0,1:T(8,128)(2,1)S(1)}, /*index=5*/s32[]{:T(128)}) while((s32[]{:T(128)}, bf16[2,512,16]{1,2,0:T(8,128)(2,1)S(1)}, bf16[2,512,16]{1,2,0:T(8,128)(2,1)S(1)}, ...), condition=%wide.region_6.6_spmd, body=%wide.region_3.5_spmd.sunk | while | flops 36191232 | bytes 6400077 | solution.py:31
  29.0 0.5 fusion.43
  29.6 0.5 fusion.44
  30.1 0.5 fusion.45
  30.6 0.5 fusion.43
  31.1 0.5 fusion.44
  31.6 0.5 fusion.45
  32.3 3.1 %while.22 = (s32[]{:T(128)}, bf16[2,512,16]{1,2,0:T(8,128)(2,1)S(1)}, bf16[2,512,16]{1,2,0:T(8,128)(2,1)S(1)}, bf16[1024,16]{0,1:T(8,128)(2,1)S(1)}, bf16[1024,16]{0,1:T(8,128)(2,1)S(1)}, /*index=5*/s32[]{:T(128)}) while((s32[]{:T(128)}, bf16[2,512,16]{1,2,0:T(8,128)(2,1)S(1)}, bf16[2,512,16]{1,2,0:T(8,128)(2,1)S(1)}, ...), condition=%wide.region_6.6_spmd, body=%wide.region_3.5_spmd.sunk | while | flops 36191232 | bytes 6400077 | solution.py:31
  32.3 0.5 fusion.43
  32.8 0.5 fusion.44
  33.3 0.5 fusion.45
  33.8 0.5 fusion.43
  34.4 0.5 fusion.44
  34.9 0.5 fusion.45
  35.5 3.1 %while.22 = (s32[]{:T(128)}, bf16[2,512,16]{1,2,0:T(8,128)(2,1)S(1)}, bf16[2,512,16]{1,2,0:T(8,128)(2,1)S(1)}, bf16[1024,16]{0,1:T(8,128)(2,1)S(1)}, bf16[1024,16]{0,1:T(8,128)(2,1)S(1)}, /*index=5*/s32[]{:T(128)}) while((s32[]{:T(128)}, bf16[2,512,16]{1,2,0:T(8,128)(2,1)S(1)}, bf16[2,512,16]{1,2,0:T(8,128)(2,1)S(1)}, ...), condition=%wide.region_6.6_spmd, body=%wide.region_3.5_spmd.sunk | while | flops 36191232 | bytes 6400077 | solution.py:31
  35.6 0.5 fusion.43
  36.1 0.5 fusion.44
  36.6 0.5 fusion.45
  37.1 0.5 fusion.43
  37.6 0.5 fusion.44
  38.1 0.5 fusion.45
  38.8 3.1 %while.22 = (s32[]{:T(128)}, bf16[2,512,16]{1,2,0:T(8,128)(2,1)S(1)}, bf16[2,512,16]{1,2,0:T(8,128)(2,1)S(1)}, bf16[1024,16]{0,1:T(8,128)(2,1)S(1)}, bf16[1024,16]{0,1:T(8,128)(2,1)S(1)}, /*index=5*/s32[]{:T(128)}) while((s32[]{:T(128)}, bf16[2,512,16]{1,2,0:T(8,128)(2,1)S(1)}, bf16[2,512,16]{1,2,0:T(8,128)(2,1)S(1)}, ...), condition=%wide.region_6.6_spmd, body=%wide.region_3.5_spmd.sunk | while | flops 36191232 | bytes 6400077 | solution.py:31
  38.8 0.5 fusion.43
  39.4 0.5 fusion.44
  39.9 0.5 fusion.45
  40.3 0.5 fusion.43
  40.9 0.5 fusion.44
  41.4 0.5 fusion.45
  42.1 3.1 %while.22 = (s32[]{:T(128)}, bf16[2,512,16]{1,2,0:T(8,128)(2,1)S(1)}, bf16[2,512,16]{1,2,0:T(8,128)(2,1)S(1)}, bf16[1024,16]{0,1:T(8,128)(2,1)S(1)}, bf16[1024,16]{0,1:T(8,128)(2,1)S(1)}, /*index=5*/s32[]{:T(128)}) while((s32[]{:T(128)}, bf16[2,512,16]{1,2,0:T(8,128)(2,1)S(1)}, bf16[2,512,16]{1,2,0:T(8,128)(2,1)S(1)}, ...), condition=%wide.region_6.6_spmd, body=%wide.region_3.5_spmd.sunk | while | flops 36191232 | bytes 6400077 | solution.py:31
  42.1 0.5 fusion.43
  42.6 0.5 fusion.44
  43.1 0.5 fusion.45
  43.6 0.5 fusion.43
  44.2 0.5 fusion.44
  44.7 0.5 fusion.45
  45.3 3.1 %while.22 = (s32[]{:T(128)}, bf16[2,512,16]{1,2,0:T(8,128)(2,1)S(1)}, bf16[2,512,16]{1,2,0:T(8,128)(2,1)S(1)}, bf16[1024,16]{0,1:T(8,128)(2,1)S(1)}, bf16[1024,16]{0,1:T(8,128)(2,1)S(1)}, /*index=5*/s32[]{:T(128)}) while((s32[]{:T(128)}, bf16[2,512,16]{1,2,0:T(8,128)(2,1)S(1)}, bf16[2,512,16]{1,2,0:T(8,128)(2,1)S(1)}, ...), condition=%wide.region_6.6_spmd, body=%wide.region_3.5_spmd.sunk | while | flops 36191232 | bytes 6400077 | solution.py:31
  45.3 0.5 fusion.43
  45.9 0.5 fusion.44
  46.4 0.5 fusion.45
  46.9 0.5 fusion.43
  47.4 0.5 fusion.44
  47.9 0.5 fusion.45
  48.5 1.6 %copy.26 = bf16[6,1024,16]{2,0,1:T(8,128)(2,1)S(1)} copy(bf16[6,1024,16]{1,2,0:T(8,128)(2,1)S(1)} %get-tuple-element.49) | data formatting | bytes 393216 | tf_op jit(solution)/shard_map/while | solution.py:34
  50.1 1.5 %bitcast_bitcast_fusion = bf16[1024,1,6,16]{3,2,1,0:T(8,128)(2,1)} fusion(bf16[6,1024,16]{2,0,1:T(8,128)(2,1)S(1)} %copy.26), kind=kLoop, calls=%fused_computation.39 | loop fusion | bytes 393216
  51.6 2.9 %reshape.60 = bf16[8,2,6144]{2,1,0:T(2,128)(2,1)S(1)} reshape(bf16[1024,1,6,16]{3,2,1,0:T(8,128)(2,1)} %bitcast_bitcast_fusion) | data formatting | bytes 393216
  54.5 11.6 %all_to_all.30 = bf16[8,2,6144]{2,1,0:T(2,128)(2,1)S(1)} all-to-all(bf16[8,2,6144]{2,1,0:T(2,128)(2,1)S(1)} %reshape.60), channel_id=1, replica_groups=mesh['groups'=2,'lon'=8,'lat'=2] {'lon'}, dimensions={0} | all-to-all | bytes 393216 | tf_op jit(solution)/shard_map/all_to_all | solution.py:67
  66.1 1.9 %reshape.61 = bf16[1024,1,6,16]{3,2,1,0:T(8,128)(2,1)S(1)} reshape(bf16[8,2,6144]{2,1,0:T(2,128)(2,1)S(1)} %all_to_all.30) | data formatting | bytes 393216
  68.1 1.3 %copy.31 = bf16[1,6,8,128,16]{3,2,4,1,0:T(8,128)(2,1)S(1)} copy(bf16[1,6,8,128,16]{4,1,3,2,0:T(8,128)(2,1)S(1)} %bitcast.68) | data formatting | bytes 393216 | tf_op jit(solution)/shard_map/all_to_all | solution.py:67
  69.4 0.0 copy-done.1
  69.4 0.0 copy-done.2
  69.4 0.9 %fusion.11 = bf16[6,128,128]{2,1,0:T(8,128)(2,1)} fusion(bf16[6,128,128]{1,2,0:T(8,128)(2,1)S(1)} %bitcast.75, bf16[6,128,128]{2,1,0:T(8,128)(2,1)S(1)} %copy-done.1, bf16[128,128]{1,0:T(8,128)(2,1)S(1)} %copy-done.2), kind=kOutput, calls=%fused_computation.16 | convolution fusion | flops 25460736 | bytes 622592 | tf_op jit(solution)/shard_map/dot_general | solution.py:70
  (51 shorter events, 0.7 us)
Async XLA Ops:
  0.0 2.4 %copy-start = (bf16[128,384]{1,0:T(8,128)(2,1)S(1)}, bf16[128,384]{1,0:T(8,128)(2,1)}, u32[]{:S(2)}) copy-start(bf16[128,384]{1,0:T(8,128)(2,1)} %param.10) | copy-start | bytes 294916
  5.3 23.2 %all-to-all-start = ((bf16[8,6,128,48]{2,3,1,0:T(8,128)(2,1)}), bf16[8,6,128,48]{2,3,1,0:T(8,128)(2,1)S(1)}, u32[]{:S(2)}, u32[]{:S(2)}) async-start(bf16[8,6,128,48]{2,3,1,0:T(8,128)(2,1)} %bitcast.8), calls=%async_computation | async-start | bytes 1179648 | tf_op jit(solution)/shard_map/all_to_all | solution.py:66
  66.1 3.3 %copy-start.1 = (bf16[6,128,128]{2,1,0:T(8,128)(2,1)S(1)}, bf16[6,128,128]{2,1,0:T(8,128)(2,1)}, u32[]{:S(2)}) copy-start(bf16[6,128,128]{2,1,0:T(8,128)(2,1)} %param.8) | copy-start | bytes 589828
  66.1 3.3 %copy-start.2 = (bf16[128,128]{1,0:T(8,128)(2,1)S(1)}, bf16[128,128]{1,0:T(8,128)(2,1)}, u32[]{:S(2)}) copy-start(bf16[128,128]{1,0:T(8,128)(2,1)} %param.11) | copy-start | bytes 98308
where the time goes:
time: 70.6 us; the launch traced here: 70.3 us
  waiting for transfers between devices  15.9 us (23%)
  matrix products  14.6 us (21%)
  blocking collectives  11.6 us (16%)
  local copies, waits for them, and re-layouts  10.9 us (15%)
  other arithmetic  9.4 us (13%)
  starting transfers between devices  7.31 us (10%)
    all_to_all x1, waiting for transfers between devices, body(): lax.all_to_all(stacked, 'lon', split_axis=0, concat_axis=2, tiled=True)  15.9 us
    all_to_all x1, blocking collectives, body(): lax.all_to_all(results, 'lon', split_axis=2, concat_axis=0, tiled=True)  11.6 us
    all_to_all x1, starting transfers between devices, body(): lax.all_to_all(stacked, 'lon', split_axis=0, concat_axis=2, tiled=True)  7.31 us
    dot_general x12, matrix products, one_block(): jnp.dot(query_block, item_keys.T, preferred_element_type=jnp.float32)  6.53 us
    unnamed x9, local copies, waits for them, and re-layouts  6.34 us
    reduce_sum x12, other arithmetic, one_block(): totals = jnp.sum(expd, axis=-1, keepdims=True)  6.16 us
    dot_general x12, matrix products, one_block(): jnp.dot(expd.astype(jnp.bfloat16), item_values, preferred_element_type=jn...  5.77 us
    while x1, local copies, waits for them, and re-layouts, attend_items(): results = lax.map(one_item, flat)  1.61 us
  transfers between devices with their start and end apart: 1, of which 1 were waited for; matrix products, arithmetic and copies ran while one was open for 0% of the time, Pallas kernels for 0%

commit v1 on v0

v1 whole, which is shorter than its diff:
```python
import functools
import math

import jax
import jax.numpy as jnp
from jax import lax
from jax.experimental import pallas as pl
from jax.experimental.pallas import tpu as pltpu
from jax.sharding import PartitionSpec as P

HEADS = 8
LOG2E = math.log2(math.e)
MESH = pl.DeviceIdType.MESH


def dot(a, b, contract):
    return lax.dot_general(a, b, ((contract[:1], contract[1:]), ((), ())), preferred_element_type=jnp.float32)


def kernel(n, per, slots, fields_ref, gain_ref, wqkv_ref, wout_ref, out_ref,
           normed, whole, w_t, scores_a, scores_b, mixed, returned,
           send1, recv1, send2, recv2):
    me = lax.axis_index("lon")
    rows, cells, width = fields_ref.shape
    head_width = width // HEADS
    total = n * cells
    block = math.gcd(total, 256)
    chunk = math.gcd(total, 256)

    barrier = pltpu.get_barrier_semaphore()
    for k in range(1, n):
        pl.semaphore_signal(barrier, inc=1, device_id={"lon": lax.rem(me + k, n)}, device_id_type=MESH)

    gain = gain_ref[...]
    for r in range(rows):
        inputs = fields_ref[r].astype(jnp.float32)
        center = jnp.mean(inputs, axis=-1, keepdims=True)
        spread = jnp.mean((inputs - center) ** 2, axis=-1, keepdims=True)
        normed[r] = ((inputs - center) * lax.rsqrt(spread + 1e-05) * gain).astype(jnp.bfloat16)

    def first_row(d):
        return (d * per) // HEADS

    def last_row(d):
        return (d * per + per - 1) // HEADS

    pl.semaphore_wait(barrier, n - 1)

    def forward(j, k):
        d = lax.rem(me + k, n)
        return d, pltpu.make_async_remote_copy(
            src_ref=normed.at[first_row(d) + j],
            dst_ref=whole.at[j, me],
            send_sem=send1.at[j, k],
            recv_sem=recv1.at[j, me],
            device_id={"lon": d},
            device_id_type=MESH,
        )

    for j in range(slots):
        for k in range(1, n):
            d, copy = forward(j, k)

            @pl.when(first_row(d) + j <= last_row(d))
            def _():
                copy.start()

    for j in range(slots):
        @pl.when(first_row(me) + j <= last_row(me))
        def _():
            whole[j, me] = normed[first_row(me) + j]

    w_t[...] = wqkv_ref[...].astype(jnp.float32).T.astype(jnp.bfloat16)

    def back(t, k):
        d = lax.rem(me + k, n)
        return pltpu.make_async_remote_copy(
            src_ref=mixed.at[t, d],
            dst_ref=returned.at[me * per + t],
            send_sem=send2.at[t, k],
            recv_sem=recv2.at[me * per + t],
            device_id={"lon": d},
            device_id_type=MESH,
        )

    def one_item(t, carry):
        item = me * per + t
        head = lax.rem(item, HEADS)
        slot = item // HEADS - first_row(me)

        @pl.when((t == 0) | (head == 0))
        def _():
            for k in range(1, n):
                src = lax.rem(me + k, n)
                pltpu.make_async_remote_copy(
                    src_ref=normed.at[0],
                    dst_ref=whole.at[slot, src],
                    send_sem=send1.at[0, 0],
                    recv_sem=recv1.at[slot, src],
                    device_id={"lon": src},
                    device_id_type=MESH,
                ).wait_recv()

        cell_rows = whole[slot].reshape(total, width)

        def weight(part):
            start = pl.multiple_of(part * width + head * head_width, head_width)
            return w_t[pl.ds(start, head_width), :]

        w_k = weight(1)
        q_t = (dot(weight(0), cell_rows, (1, 1)) * (1.0 / math.sqrt(head_width))).astype(jnp.bfloat16)
        q_t = q_t.astype(jnp.float32) * LOG2E
        q_hi = q_t.astype(jnp.bfloat16)
        q_lo = (q_t - q_hi.astype(jnp.float32)).astype(jnp.bfloat16)
        q_pair = jnp.concatenate([q_hi, q_lo], axis=0)
        keys = dot(cell_rows, jnp.concatenate([w_k, w_k], axis=0), (1, 1)).astype(jnp.bfloat16)
        v_t = dot(weight(2), cell_rows, (1, 1)).astype(jnp.bfloat16)

        buffers = (scores_a, scores_b)

        def first_pass(b):
            q_block = q_pair[:, b * block:(b + 1) * block]
            highest = None
            for c in range(total // chunk):
                s = dot(keys[c * chunk:(c + 1) * chunk], q_block, (1, 0))
                buffers[b % 2][pl.ds(c * chunk, chunk), :] = s
                part = jnp.max(s.reshape(chunk // 8, 8, block), axis=0)
                highest = part if highest is None else jnp.maximum(highest, part)
            return jnp.max(highest, axis=0, keepdims=True)

        def second_pass(b, highest):
            sums = jnp.zeros((8, block), jnp.float32)
            acc = jnp.zeros((head_width, block), jnp.float32)
            for c in range(total // chunk):
                p = jnp.exp2(buffers[b % 2][pl.ds(c * chunk, chunk), :] - highest)
                sums = sums + jnp.sum(p.reshape(chunk // 8, 8, block), axis=0)
                acc = acc + dot(v_t[:, c * chunk:(c + 1) * chunk], p.astype(jnp.bfloat16), (1, 0))
            return (acc / jnp.sum(sums, axis=0, keepdims=True)).astype(jnp.bfloat16)

        blocks = total // block
        highest = first_pass(0)
        for b in range(blocks):
            following = first_pass(b + 1) if b + 1 < blocks else None
            done = second_pass(b, highest)
            highest = following
            for s in range(block // cells):
                mixed[t, b * (block // cells) + s] = done[:, s * cells:(s + 1) * cells]

        returned[item] = mixed[t, me]
        for k in range(1, n):
            back(t, k).start()
        return carry

    lax.fori_loop(0, per, one_item, 0)

    def finish(t, carry):
        for k in range(1, n):
            src = lax.rem(me + k, n)
            pltpu.make_async_remote_copy(
                src_ref=mixed.at[0, 0],
                dst_ref=returned.at[src * per + t],
                send_sem=send2.at[t, k],
                recv_sem=recv2.at[src * per + t],
                device_id={"lon": src},
                device_id_type=MESH,
            ).wait_recv()
        return carry

    lax.fori_loop(0, per, finish, 0)

    for r in range(rows):
        att_t = returned[pl.ds(r * HEADS, HEADS)].reshape(width, cells)
        update = dot(att_t, wout_ref[...], (0, 0))
        out_ref[r] = (fields_ref[r].astype(jnp.float32) + update).astype(jnp.bfloat16)

    for j in range(slots):
        for k in range(1, n):
            d, copy = forward(j, k)

            @pl.when(first_row(d) + j <= last_row(d))
            def _():
                copy.wait_send()

    def sent(t, carry):
        for k in range(1, n):
            back(t, k).wait_send()
        return carry

    lax.fori_loop(0, per, sent, 0)


def solution(mesh):
    n = mesh.shape["lon"]

    def body(fields, norm_gain, w_qkv, w_out):
        rows, cells, width = fields.shape
        per = rows * HEADS // n
        slots = max((d * per + per - 1) // HEADS - (d * per) // HEADS + 1 for d in range(n))
        total = n * cells
        block = math.gcd(total, 256)
        return pl.pallas_call(
            functools.partial(kernel, n, per, slots),
            out_shape=jax.ShapeDtypeStruct(fields.shape, fields.dtype),
            in_specs=[pl.BlockSpec(memory_space=pltpu.VMEM)] * 4,
            out_specs=pl.BlockSpec(memory_space=pltpu.VMEM),
            scratch_shapes=[
                pltpu.VMEM((rows, cells, width), jnp.bfloat16),
                pltpu.VMEM((slots, n, cells, width), jnp.bfloat16),
                pltpu.VMEM((3 * width, width), jnp.bfloat16),
                pltpu.VMEM((total, block), jnp.float32),
                pltpu.VMEM((total, block), jnp.float32),
                pltpu.VMEM((per, n, width // HEADS, cells), jnp.bfloat16),
                pltpu.VMEM((rows * HEADS, width // HEADS, cells), jnp.bfloat16),
                pltpu.SemaphoreType.DMA((slots, n)),
                pltpu.SemaphoreType.DMA((slots, n)),
                pltpu.SemaphoreType.DMA((per, n)),
                pltpu.SemaphoreType.DMA((rows * HEADS,)),
            ],
            compiler_params=pltpu.CompilerParams(collective_id=0, has_side_effects=True),
        )(fields, norm_gain.reshape(1, width), w_qkv, w_out)

    return jax.shard_map(
        body,
        mesh=mesh,
        in_specs=(P(("groups", "lat"), "lon", None), P(), P(), P()),
        out_specs=P(("groups", "lat"), "lon", None),
        check_vma=False,
    )
```

time: 70.6 us -> 34.4 us (0.49)
  Pallas kernels: 0 us -> 32.6 us
  waiting for transfers between devices: 15.9 us -> 0 us
  matrix products: 14.6 us -> 0 us
  blocking collectives: 11.6 us -> 0 us
  other arithmetic: 9.4 us -> 0 us
  local copies, waits for them, and re-layouts: 10.9 us -> 1.62 us
  starting transfers between devices: 7.31 us -> 0 us
    pallas_call x0 -> x1, Pallas kernels: none -> 32.6 us  [body(): pl.pallas_call(functools.partial(kernel, n, per, slots), out_shape=jax.Sh...]
    all_to_all x1 -> x0, waiting for transfers between devices: 15.9 us -> none  [body(): lax.all_to_all(stacked, 'lon', split_axis=0, concat_axis=2, tiled=True)]
    dot_general x26 -> x0, matrix products: 14.6 us -> none  [the longest x12 6.53 us: one_block(): jnp.dot(query_block, item_keys.T, preferred_element_type=jnp.float32)]
    all_to_all x1 -> x0, blocking collectives: 11.6 us -> none  [body(): lax.all_to_all(results, 'lon', split_axis=2, concat_axis=0, tiled=True)]
    reduce_sum x14 -> x0, other arithmetic: 8.49 us -> none  [the longest x12 6.16 us: one_block(): totals = jnp.sum(expd, axis=-1, keepdims=True)]
    all_to_all x1 -> x0, starting transfers between devices: 7.31 us -> none  [body(): lax.all_to_all(stacked, 'lon', split_axis=0, concat_axis=2, tiled=True)]
    unnamed x9 -> x1, local copies, waits for them, and re-layouts: 6.34 us -> 1.62 us
    while x7 -> x0, local copies, waits for them, and re-layouts: 1.85 us -> none  [the longest x1 1.61 us: attend_items(): results = lax.map(one_item, flat)]
  transfers between devices with their start and end apart: 1 -> 0, of which waited for: 1 -> 0; matrix products, arithmetic and copies ran while one was open for 0% -> 0% of each run, Pallas kernels for 0% -> 0%
where the time goes in v1:
time: 34.4 us; the launch traced here: 34.3 us
  Pallas kernels  32.6 us (95%)
  local copies, waits for them, and re-layouts  1.62 us (5%)
    pallas_call x1, Pallas kernels, body(): pl.pallas_call(functools.partial(kernel, n, per, slots), out_shape=jax.Sh...  32.6 us
    unnamed x1, local copies, waits for them, and re-layouts  1.62 us

profile of v1, /device:TPU:0, one launch (start us, length us, event | category | flops | bytes accessed | tf_op | source)
XLA Modules:
  0.0 34.3 jit_solution(3152247416737881621)
XLA Ops:
  0.0 32.6 %shard_map.46 = bf16[6,128,128]{2,1,0:T(8,128)(2,1)} custom-call(bf16[6,128,128]{2,1,0:T(8,128)(2,1)} %fields_ref.1, f32[1,128]{1,0:T(1,128)} %bitcast.1, bf16[128,384]{1,0:T(8,128)(2,1)} %wqkv_ref.1, bf16[128,128]{1,0:T(8,128)(2,1)} %wout_ref.1), custom_call_target="tpu_custom_call" | custom-call | tf_op jit(solution)/shard_map/pallas_call | solution.py:201
  32.7 1.6 %copy.6 = bf16[6,128,128]{2,1,0:T(8,128)(2,1)} copy(bf16[6,128,128]{2,1,0:T(8,128)(2,1)} %shard_map.46) | data formatting | bytes 393216

commit v2 on v1

--- a/solution.py
+++ b/solution.py
@@ -18,14 +18,24 @@
 
 
 def kernel(n, per, slots, fields_ref, gain_ref, wqkv_ref, wout_ref, out_ref,
-           normed, whole, w_t, scores_a, scores_b, mixed, returned,
+           normed, whole, w_t, scores_a, scores_b, scores_c, q_s, k_s, v_s,
+           mixed, returned,
            send1, recv1, send2, recv2):
     me = lax.axis_index("lon")
     rows, cells, width = fields_ref.shape
     head_width = width // HEADS
     total = n * cells
-    block = math.gcd(total, 256)
+    block = math.gcd(total, 512)
     chunk = math.gcd(total, 256)
+
+    def partner(k):
+        if n & (n - 1):
+            return lax.rem(me + n - k, n)
+        mate = 0
+        for bit in range(n.bit_length() - 1):
+            own = lax.rem(me // (1 << bit), 2)
+            mate = mate + ((1 - own) if (k >> bit) & 1 else own) * (1 << bit)
+        return mate
 
     barrier = pltpu.get_barrier_semaphore()
     for k in range(1, n):
@@ -47,7 +57,7 @@
     pl.semaphore_wait(barrier, n - 1)
 
     def forward(j, k):
-        d = lax.rem(me + k, n)
+        d = partner(k)
         return d, pltpu.make_async_remote_copy(
             src_ref=normed.at[first_row(d) + j],
             dst_ref=whole.at[j, me],
@@ -58,7 +68,7 @@
         )
 
     for j in range(slots):
-        for k in range(1, n):
+        for k in range(n - 1, 0, -1):
             d, copy = forward(j, k)
 
             @pl.when(first_row(d) + j <= last_row(d))
@@ -73,7 +83,7 @@
     w_t[...] = wqkv_ref[...].astype(jnp.float32).T.astype(jnp.bfloat16)
 
     def back(t, k):
-        d = lax.rem(me + k, n)
+        d = partner(k)
         return pltpu.make_async_remote_copy(
             src_ref=mixed.at[t, d],
             dst_ref=returned.at[me * per + t],
@@ -83,25 +93,21 @@
             device_id_type=MESH,
         )
 
-    def one_item(t, carry):
-        item = me * per + t
+    def wait_slot(slot):
+        for k in range(1, n):
+            src = lax.rem(me + k, n)
+            pltpu.make_async_remote_copy(
+                src_ref=normed.at[0],
+                dst_ref=whole.at[slot, src],
+                send_sem=send1.at[0, 0],
+                recv_sem=recv1.at[slot, src],
+                device_id={"lon": src},
+                device_id_type=MESH,
+            ).wait_recv()
+
+    def project(item):
         head = lax.rem(item, HEADS)
-        slot = item // HEADS - first_row(me)
-
-        @pl.when((t == 0) | (head == 0))
-        def _():
-            for k in range(1, n):
-                src = lax.rem(me + k, n)
-                pltpu.make_async_remote_copy(
-                    src_ref=normed.at[0],
-                    dst_ref=whole.at[slot, src],
-                    send_sem=send1.at[0, 0],
-                    recv_sem=recv1.at[slot, src],
-                    device_id={"lon": src},
-                    device_id_type=MESH,
-                ).wait_recv()
-
-        cell_rows = whole[slot].reshape(total, width)
+        cell_rows = whole[item // HEADS - first_row(me)].reshape(total, width)
 
         def weight(part):
             start = pl.multiple_of(part * width + head * head_width, head_width)
@@ -112,46 +118,61 @@
         q_t = q_t.astype(jnp.float32) * LOG2E
         q_hi = q_t.astype(jnp.bfloat16)
         q_lo = (q_t - q_hi.astype(jnp.float32)).astype(jnp.bfloat16)
-        q_pair = jnp.concatenate([q_hi, q_lo], axis=0)
-        keys = dot(cell_rows, jnp.concatenate([w_k, w_k], axis=0), (1, 1)).astype(jnp.bfloat16)
-        v_t = dot(weight(2), cell_rows, (1, 1)).astype(jnp.bfloat16)
-
-        buffers = (scores_a, scores_b)
-
-        def first_pass(b):
-            q_block = q_pair[:, b * block:(b + 1) * block]
-            highest = None
-            for c in range(total // chunk):
-                s = dot(keys[c * chunk:(c + 1) * chunk], q_block, (1, 0))
-                buffers[b % 2][pl.ds(c * chunk, chunk), :] = s
-                part = jnp.max(s.reshape(chunk // 8, 8, block), axis=0)
-                highest = part if highest is None else jnp.maximum(highest, part)
-            return jnp.max(highest, axis=0, keepdims=True)
-
-        def second_pass(b, highest):
-            sums = jnp.zeros((8, block), jnp.float32)
-            acc = jnp.zeros((head_width, block), jnp.float32)
-            for c in range(total // chunk):
-                p = jnp.exp2(buffers[b % 2][pl.ds(c * chunk, chunk), :] - highest)
-                sums = sums + jnp.sum(p.reshape(chunk // 8, 8, block), axis=0)
-                acc = acc + dot(v_t[:, c * chunk:(c + 1) * chunk], p.astype(jnp.bfloat16), (1, 0))
-            return (acc / jnp.sum(sums, axis=0, keepdims=True)).astype(jnp.bfloat16)
-
+        q_s[...] = jnp.concatenate([q_hi, q_lo], axis=0)
+        k_s[...] = dot(cell_rows, jnp.concatenate([w_k, w_k], axis=0), (1, 1)).astype(jnp.bfloat16)
+        v_s[...] = dot(weight(2), cell_rows, (1, 1)).astype(jnp.bfloat16)
+
+    def buffer(b):
+        return scores_c if b == 0 else (scores_a, scores_b)[b % 2]
+
+    def first_pass(b, queries, keys):
+        q_block = queries[:, b * block:(b + 1) * block]
+        highest = None
+        for c in range(total // chunk):
+            s = dot(keys[c * chunk:(c + 1) * chunk], q_block, (1, 0))
+            buffer(b)[pl.ds(c * chunk, chunk), :] = s
+            part = jnp.max(s.reshape(chunk // 8, 8, block), axis=0)
+            highest = part if highest is None else jnp.maximum(highest, part)
+        return jnp.max(highest, axis=0, keepdims=True)
+
+    def second_pass(b, highest, v_t):
+        sums = jnp.zeros((8, block), jnp.float32)
+        acc = jnp.zeros((head_width, block), jnp.float32)
+        for c in range(total // chunk):
+            p = jnp.exp2(buffer(b)[pl.ds(c * chunk, chunk), :] - highest)
+            sums = sums + jnp.sum(p.reshape(chunk // 8, 8, block), axis=0)
+            acc = acc + dot(v_t[:, c * chunk:(c + 1) * chunk], p.astype(jnp.bfloat16), (1, 0))
+        return (acc / jnp.sum(sums, axis=0, keepdims=True)).astype(jnp.bfloat16)
+
+    def one_item(t, highest):
+        item = me * per + t
+        after = jnp.minimum(item + 1, me * per + per - 1)
+
+        @pl.when((t + 1 < per) & (lax.rem(item + 1, HEADS) == 0))
+        def _():
+            wait_slot(after // HEADS - first_row(me))
+
+        queries, keys, v_t = q_s[...], k_s[...], v_s[...]
+        project(after)
         blocks = total // block
-        highest = first_pass(0)
         for b in range(blocks):
-            following = first_pass(b + 1) if b + 1 < blocks else None
-            done = second_pass(b, highest)
+            if b + 1 < blocks:
+                following = first_pass(b + 1, queries, keys)
+            done = second_pass(b, highest, v_t)
+            if b + 1 == blocks:
+                following = first_pass(0, q_s[...], k_s[...])
             highest = following
             for s in range(block // cells):
                 mixed[t, b * (block // cells) + s] = done[:, s * cells:(s + 1) * cells]
 
         returned[item] = mixed[t, me]
-        for k in range(1, n):
+        for k in range(n - 1, 0, -1):
             back(t, k).start()
-        return carry
-
-    lax.fori_loop(0, per, one_item, 0)
+        return highest
+
+    wait_slot(0)
+    project(me * per)
+    lax.fori_loop(0, per, one_item, first_pass(0, q_s[...], k_s[...]))
 
     def finish(t, carry):
         for k in range(1, n):
@@ -197,7 +218,7 @@
         per = rows * HEADS // n
         slots = max((d * per + per - 1) // HEADS - (d * per) // HEADS + 1 for d in range(n))
         total = n * cells
-        block = math.gcd(total, 256)
+        block = math.gcd(total, 512)
         return pl.pallas_call(
             functools.partial(kernel, n, per, slots),
             out_shape=jax.ShapeDtypeStruct(fields.shape, fields.dtype),
@@ -209,6 +230,10 @@
                 pltpu.VMEM((3 * width, width), jnp.bfloat16),
                 pltpu.VMEM((total, block), jnp.float32),
                 pltpu.VMEM((total, block), jnp.float32),
+                pltpu.VMEM((total, block), jnp.float32),
+                pltpu.VMEM((2 * width // HEADS, total), jnp.bfloat16),
+                pltpu.VMEM((total, 2 * width // HEADS), jnp.bfloat16),
+                pltpu.VMEM((width // HEADS, total), jnp.bfloat16),
                 pltpu.VMEM((per, n, width // HEADS, cells), jnp.bfloat16),
                 pltpu.VMEM((rows * HEADS, width // HEADS, cells), jnp.bfloat16),
                 pltpu.SemaphoreType.DMA((slots, n)),

time: 34.4 us -> 33.7 us (0.980)
  Pallas kernels: 32.6 us -> 31.9 us
    pallas_call x1, Pallas kernels: 32.6 us -> 31.9 us  [body(): pl.pallas_call(functools.partial(kernel, n, per, slots), out_shape=jax.Sh...]
where the time goes in v2:
time: 33.7 us; the launch traced here: 33.6 us
  Pallas kernels  31.9 us (95%)
  local copies, waits for them, and re-layouts  1.62 us (5%)
    pallas_call x1, Pallas kernels, body(): pl.pallas_call(functools.partial(kernel, n, per, slots), out_shape=jax.Sh...  31.9 us
    unnamed x1, local copies, waits for them, and re-layouts  1.62 us

profile of v2, /device:TPU:0, one launch (start us, length us, event | category | flops | bytes accessed | tf_op | source)
XLA Modules:
  0.0 33.6 jit_solution(7000151558387644698)
XLA Ops:
  0.0 31.9 %shard_map.46 = bf16[6,128,128]{2,1,0:T(8,128)(2,1)} custom-call(bf16[6,128,128]{2,1,0:T(8,128)(2,1)} %fields_ref.1, f32[1,128]{1,0:T(1,128)} %bitcast.1, bf16[128,384]{1,0:T(8,128)(2,1)} %wqkv_ref.1, bf16[128,128]{1,0:T(8,128)(2,1)} %wout_ref.1), custom_call_target="tpu_custom_call" | custom-call | tf_op jit(solution)/shard_map/pallas_call | solution.py:222
  32.0 1.6 %copy.6 = bf16[6,128,128]{2,1,0:T(8,128)(2,1)} copy(bf16[6,128,128]{2,1,0:T(8,128)(2,1)} %shard_map.46) | data formatting | bytes 393216

commit v3 on v2

--- a/solution.py
+++ b/solution.py
@@ -17,9 +17,9 @@
     return lax.dot_general(a, b, ((contract[:1], contract[1:]), ((), ())), preferred_element_type=jnp.float32)
 
 
-def kernel(n, per, slots, fields_ref, gain_ref, wqkv_ref, wout_ref, out_ref,
+def kernel(n, per, slots, fields_ref, gain_ref, wqkv_ref, returned,
            normed, whole, w_t, scores_a, scores_b, scores_c, q_s, k_s, v_s,
-           mixed, returned,
+           mixed,
            send1, recv1, send2, recv2):
     me = lax.axis_index("lon")
     rows, cells, width = fields_ref.shape
@@ -189,11 +189,6 @@
 
     lax.fori_loop(0, per, finish, 0)
 
-    for r in range(rows):
-        att_t = returned[pl.ds(r * HEADS, HEADS)].reshape(width, cells)
-        update = dot(att_t, wout_ref[...], (0, 0))
-        out_ref[r] = (fields_ref[r].astype(jnp.float32) + update).astype(jnp.bfloat16)
-
     for j in range(slots):
         for k in range(1, n):
             d, copy = forward(j, k)
@@ -219,10 +214,10 @@
         slots = max((d * per + per - 1) // HEADS - (d * per) // HEADS + 1 for d in range(n))
         total = n * cells
         block = math.gcd(total, 512)
-        return pl.pallas_call(
+        att_t = pl.pallas_call(
             functools.partial(kernel, n, per, slots),
-            out_shape=jax.ShapeDtypeStruct(fields.shape, fields.dtype),
-            in_specs=[pl.BlockSpec(memory_space=pltpu.VMEM)] * 4,
+            out_shape=jax.ShapeDtypeStruct((rows * HEADS, width // HEADS, cells), fields.dtype),
+            in_specs=[pl.BlockSpec(memory_space=pltpu.VMEM)] * 3,
             out_specs=pl.BlockSpec(memory_space=pltpu.VMEM),
             scratch_shapes=[
                 pltpu.VMEM((rows, cells, width), jnp.bfloat16),
@@ -235,14 +230,15 @@
                 pltpu.VMEM((total, 2 * width // HEADS), jnp.bfloat16),
                 pltpu.VMEM((width // HEADS, total), jnp.bfloat16),
                 pltpu.VMEM((per, n, width // HEADS, cells), jnp.bfloat16),
-                pltpu.VMEM((rows * HEADS, width // HEADS, cells), jnp.bfloat16),
                 pltpu.SemaphoreType.DMA((slots, n)),
                 pltpu.SemaphoreType.DMA((slots, n)),
                 pltpu.SemaphoreType.DMA((per, n)),
                 pltpu.SemaphoreType.DMA((rows * HEADS,)),
             ],
             compiler_params=pltpu.CompilerParams(collective_id=0, has_side_effects=True),
-        )(fields, norm_gain.reshape(1, width), w_qkv, w_out)
+        )(fields, norm_gain.reshape(1, width), w_qkv)
+        update = jnp.einsum('rcl,cd->rld', att_t.reshape(rows, width, cells), w_out, preferred_element_type=jnp.float32)
+        return (fields.astype(jnp.float32) + update).astype(jnp.bfloat16)
 
     return jax.shard_map(
         body,

time: 33.7 us -> 33.8 us (level)
  matrix products: 0 us -> 1.84 us
  local copies, waits for them, and re-layouts: 1.62 us -> 0.01 us
    dot_general x0 -> x1, matrix products: none -> 1.84 us  [body(): jnp.einsum('rcl,cd->rld', att_t.reshape(rows, width, cells), w_out, prefe...]
    unnamed x1 -> x4, local copies, waits for them, and re-layouts: 1.62 us -> 0.01 us
where the time goes in v3:
time: 33.8 us; the launch traced here: 33.6 us
  Pallas kernels  31.7 us (94%)
  matrix products  1.84 us (5%)
    pallas_call x1, Pallas kernels, body(): pl.pallas_call(functools.partial(kernel, n, per, slots), out_shape=jax.Sh...  31.7 us
    dot_general x1, matrix products, body(): jnp.einsum('rcl,cd->rld', att_t.reshape(rows, width, cells), w_out, prefe...  1.84 us

profile of v3, /device:TPU:0, one launch (start us, length us, event | category | flops | bytes accessed | tf_op | source)
XLA Modules:
  0.0 33.6 jit_solution(15125321570467408468)
XLA Ops:
  0.0 0.0 copy-start
  0.0 0.0 copy-start.1
  0.0 31.7 %shard_map.46 = bf16[48,16,128]{2,1,0:T(8,128)(2,1)} custom-call(bf16[6,128,128]{2,1,0:T(8,128)(2,1)} %fields_ref.1, f32[1,128]{1,0:T(1,128)} %bitcast.7, bf16[128,384]{1,0:T(8,128)(2,1)} %wqkv_ref.1), custom_call_target="tpu_custom_call" | custom-call | tf_op jit(solution)/shard_map/pallas_call | solution.py:217
  31.7 0.0 copy-done
  31.7 0.0 copy-done.1
  31.8 1.8 %fusion = bf16[6,128,128]{2,1,0:T(8,128)(2,1)} fusion(bf16[6,128,128]{2,1,0:T(8,128)(2,1)} %bitcast.6, bf16[6,128,128]{2,1,0:T(8,128)(2,1)S(1)} %copy-done.1, bf16[128,128]{1,0:T(8,128)(2,1)S(1)} %copy-done), kind=kOutput, calls=%fused_computation.1 | convolution fusion | flops 25460736 | bytes 622592 | tf_op jit(solution)/shard_map/rcl,cd->rld/dot_general | solution.py:240
Async XLA Ops:
  0.0 31.7 %copy-start = (bf16[128,128]{1,0:T(8,128)(2,1)S(1)}, bf16[128,128]{1,0:T(8,128)(2,1)}, u32[]{:S(2)}) copy-start(bf16[128,128]{1,0:T(8,128)(2,1)} %param.7) | copy-start | bytes 98308
  0.0 31.7 %copy-start.1 = (bf16[6,128,128]{2,1,0:T(8,128)(2,1)S(1)}, bf16[6,128,128]{2,1,0:T(8,128)(2,1)}, u32[]{:S(2)}) copy-start(bf16[6,128,128]{2,1,0:T(8,128)(2,1)} %fields_ref.1) | copy-start | bytes 589828
